TPU v7x, 16 devices: a whole 2x2x2 slice. The times are simulated.
16 devices in a mesh: data: 16 (over z, y, x, core).
Axes of the slice: x: 2, y: 2, z: 2, core: 2. Of those that a mesh axis runs over, the one named last changes fastest.
Arguments:
- tokens: bfloat16 [131072, 128], P('data')
- out_grad: bfloat16 [131072, 128], P('data')
- w_up: bfloat16 [2, 128, 512], replicated
- w_down: bfloat16 [2, 512, 128], replicated
- a_up_old: float32 [2, 128, 128], replicated
- s_up_old: float32 [2, 512, 512], replicated
- a_down_old: float32 [2, 512, 512], replicated
- s_down_old: float32 [2, 128, 128], replicated
- a_up_inv: float32 [2, 128, 128], replicated
- s_up_inv: float32 [2, 512, 512], replicated
- a_down_inv: float32 [2, 512, 512], replicated
- s_down_inv: float32 [2, 128, 128], replicated
- factor_decay: float32 [], replicated
Outputs:
- output 1: float32 [2, 128, 512], replicated
- output 2: float32 [2, 512, 128], replicated
- output 3: float32 [2, 128, 128], replicated
- output 4: float32 [2, 512, 512], replicated
- output 5: float32 [2, 512, 512], replicated
- output 6: float32 [2, 128, 128], replicated
All inputs are finite; a program needn't handle non-finite values.
Results may differ from a plain program's by a relative error of at most 0.00179582.
Values are sent between devices in bfloat16 or wider.
A program may use at most 1 GiB of HBM per device.

v0:
```python
import jax
import jax.numpy as jnp
from jax import lax
from jax.experimental import pallas as pl
from jax.experimental.pallas import tpu as pltpu
from jax.sharding import PartitionSpec as P

BF = jnp.bfloat16
F32 = jnp.float32
MESH = pl.DeviceIdType.MESH
HIGH = lax.Precision.HIGHEST
C0 = 0.7978845608028654
CA = C0 * 0.044715
TILE = 512
CHUNK = 256
STRIDE = {"c": 1, "x": 2, "y": 4, "z": 8}
ORDERS = ("cxyz", "cyzx", "czxy")

KEPT = {"S": [(r, c) for c in range(4) for r in range(c, 4)],
        "H": [(0, 0), (1, 0), (1, 1), (2, 2), (3, 2), (3, 3), (0, 2), (1, 2), (0, 3), (1, 3)]}


def tri(kind, b):
    return [(kind, b, r, c) for r, c in KEPT[kind]]


def row(kind, b):
    return [(kind, b, 0, c) for c in range(4)]


GROUPS = (
    (3, tri("H", 0)),
    (6, row("U", 1) + row("D", 1) + [("A", 1, 0, 0), ("Q", 1, 0, 0)] + tri("S", 1) + tri("H", 1)),
    (6, row("U", 0) + row("D", 0) + [("A", 0, 0, 0), ("Q", 0, 0, 0)] + tri("S", 0)),
)
SLOT = {}
PIECES = []
GROUP_PIECES = []
for _count, _blocks in GROUPS:
    _members = []
    for _n in range(_count):
        _size = -(-len(_blocks) // (_count - _n))
        _members.append(len(PIECES))
        PIECES.append((ORDERS[_n % 3], 128 * len(SLOT), 128 * _size))
        for _block in _blocks[:_size]:
            SLOT[_block] = 128 * len(SLOT)
        _blocks = _blocks[_size:]
    GROUP_PIECES.append(_members)
TOTAL_ROWS = 128 * len(SLOT)


def mm(a, b):
    return lax.dot_general(a, b, (((1,), (0,)), ((), ())), preferred_element_type=F32)


def nt(a, b):
    return lax.dot_general(a, b, (((1,), (1,)), ((), ())), preferred_element_type=F32)


def fine(a, b, ca, cb):
    return lax.dot_general(a, b, (((ca,), (cb,)), ((), ())), precision=HIGH, preferred_element_type=F32)


def rounded(x):
    return x.astype(BF).astype(F32)


def gelu_pair(z):
    sq = z * z
    cub = CA * sq
    base = cub + C0
    half = 0.5 * jnp.tanh(z * base) + 0.5
    hid = z * half
    slope = half + hid * ((base + (cub + cub)) * (2.0 - (half + half)))
    return hid, slope


def weave(first, second):
    done = 0
    for n, step in enumerate(first):
        step()
        while done < len(second) and (done + 1) * len(first) <= (n + 1) * len(second):
            second[done]()
            done += 1
    for step in second[done:]:
        step()


def body(axis_size, rows, tok_hbm, og_hbm, wu, wd, rho, old_hbm, inv_hbm, outs,
         tok, og, hid0, slope0, grad0, tiles, wut, wdt, acc_a, acc_b, acc_c, acc_d, part, recv, total, res,
         load_sem, out_sem, send_sem, recv_sem):
    me = lax.axis_index("data")
    bit = {d: (me // s) % 2 for d, s in STRIDE.items()}
    peer = {d: me + s - 2 * s * bit[d] for d, s in STRIDE.items()}
    count = rows // (2 * TILE)
    scale = 1.0 / (axis_size * rows)

    def tok_load(n):
        here = pl.ds(pl.multiple_of(n * (2 * TILE), 2 * TILE), 2 * TILE)
        return pltpu.make_async_copy(tok_hbm.at[here, :], tok.at[here, :], load_sem.at[n])

    og_load = pltpu.make_async_copy(og_hbm, og, load_sem.at[count])

    def place(n, b):
        if n % 4 in (1, 2):
            at = 512 * (4 * (n // 4) + 2 * (n % 4 - 1) + b)
            return slice(0, 512), slice(at, at + 512)
        at = 4096 + 128 * (4 * (n // 4) + 2 * (n % 4 == 3) + b)
        return slice(0, 128), slice(at, at + 128)

    late_loads = []
    for n, src in enumerate(tuple(old_hbm) + tuple(inv_hbm)):
        for b in range(2):
            at = place(n, b)
            late_loads.append(pltpu.make_async_copy(src.at[b], slope0.at[at[0], at[1]], load_sem.at[count + 1 + 2 * n + b]))

    def spot(piece, stage):
        order, base, size = PIECES[piece]
        at = base
        for s in range(stage):
            at = at + bit[order[s]] * (size >> (s + 1))
        return at

    def inbox(piece, stage):
        _, base, size = PIECES[piece]
        return base - base // 16 + sum(size >> (s + 1) for s in range(stage))

    def halving(piece, stage):
        order, _, size = PIECES[piece]
        half = size >> (stage + 1)
        away = pl.multiple_of(spot(piece, stage) + (1 - bit[order[stage]]) * half, 8)
        return pltpu.make_async_remote_copy(
            src_ref=part.at[pl.ds(away, half), :], dst_ref=recv.at[pl.ds(inbox(piece, stage), half), :],
            send_sem=send_sem.at[0, stage, piece], recv_sem=recv_sem.at[0, stage, piece],
            device_id=(peer[order[stage]],), device_id_type=MESH)

    def doubling(piece, stage):
        order, _, size = PIECES[piece]
        half = size >> (stage + 1)
        at = pl.multiple_of(spot(piece, stage + 1), 8)
        return pltpu.make_async_remote_copy(
            src_ref=total.at[pl.ds(at, half), :], dst_ref=total.at[pl.ds(at, half), :],
            send_sem=send_sem.at[1, stage, piece], recv_sem=recv_sem.at[1, stage, piece],
            device_id=(peer[order[stage]],), device_id_type=MESH)

    def tick(group, step):
        for piece in GROUP_PIECES[group]:
            order, _, size = PIECES[piece]
            if step == 0:
                halving(piece, 0).start()
            elif step < 4:
                stage = step - 1
                halving(piece, stage).wait_recv()
                at, box, half = spot(piece, step), inbox(piece, stage), size >> (step + 1)
                keep = bit[order[step]] * half
                for shift in (half - keep, keep):
                    here = pl.ds(pl.multiple_of(at + shift, 8), half)
                    there = pl.ds(pl.multiple_of(box + shift, 8), half)
                    part[here, :] = part[here, :] + recv[there, :]
                halving(piece, step).start()
            elif step == 4:
                halving(piece, 3).wait_recv()
                box, half = inbox(piece, 3), size >> 4
                here = pl.ds(pl.multiple_of(spot(piece, 4), 8), half)
                total[here, :] = part[here, :] + recv[box:box + half, :]
                doubling(piece, 3).start()
            else:
                doubling(piece, 8 - step).wait_recv()
                if step < 8:
                    doubling(piece, 7 - step).start()

    def near(n):
        return pl.ds(pl.multiple_of(n * TILE, TILE), TILE)

    def acts0(tile, n):
        kept = {}

        def start():
            kept["u"] = tok[near(n), :].T

        def chunk(f):
            def step():
                hid, slope = gelu_pair(rounded(mm(wut[0, f:f + CHUNK, :], kept["u"])))
                hid = hid.astype(BF)
                tile[768 + f:768 + f + CHUNK, :] = hid
                hid0[f:f + CHUNK, near(n)] = hid
                slope0[f:f + CHUNK, near(n)] = slope
            return step

        return [start] + [chunk(f) for f in range(0, 512, CHUNK)]

    def sums0(tile):
        def one():
            acc_a[0, 0:512, :] += nt(tile[768:1280, :], tile[1024:1280, :])

        def two():
            acc_b[0, 0:256, :] += nt(tile[768:1024, :], tile[768:1024, :])

        return [one, two]

    def acts1(tile, n):
        kept = {}

        def start():
            kept["q"] = og[near(n), :].T
            kept["u"] = mm(wdt[...], hid0[:, near(n)]).astype(BF)
            tile[512:640, :] = kept["u"]
            tile[640:768, :] = kept["q"]

        def chunk(f):
            def step():
                hid, slope = gelu_pair(rounded(mm(wut[1, f:f + CHUNK, :], kept["u"])))
                tile[768 + f:768 + f + CHUNK, :] = hid.astype(BF)
                tile[f:f + CHUNK, :] = (rounded(mm(wd[1, f:f + CHUNK, :], kept["q"])) * slope).astype(BF)
            return step

        def end():
            grad0[:, near(n)] = mm(wu[1], tile[0:512, :]).astype(BF)

        return [start] + [chunk(f) for f in range(0, 512, CHUNK)] + [end]

    def left_sums(tile, k):
        def one():
            acc_a[k] += nt(tile[0:640, :], tile[0:256, :])

        def two():
            acc_b[k] += nt(tile[256:640, :], tile[256:512, :])

        def three():
            acc_c[...] += nt(tile[512:768, :], tile[512:768, :])

        return [one, two, three]

    def sums1(tile):
        def one():
            acc_a[1] += nt(tile[640:1280, :], tile[1024:1280, :])

        def two():
            acc_b[1] += nt(tile[640:1024, :], tile[768:1024, :])

        return left_sums(tile, 0) + [one, two]

    def acts2(tile, n):
        kept = {}

        def start():
            tile[512:640, :] = tok[near(n), :].T
            tile[640:768, :] = grad0[:, near(n)]

        def chunk(f):
            def step():
                back = rounded(mm(wd[0, f:f + CHUNK, :], grad0[:, near(n)]))
                tile[f:f + CHUNK, :] = (back * slope0[f:f + CHUNK, near(n)]).astype(BF)
            return step

        return [start] + [chunk(f) for f in range(0, 512, CHUNK)]

    def sums2(tile, n):
        def one():
            acc_d[...] += nt(tile[640:768, :], hid0[:, near(n)])

        return left_sums(tile, 0) + [one]

    def phase(acts, sums, ticks):
        for acc in (acc_a, acc_b, acc_c, acc_d):
            acc[...] = jnp.zeros_like(acc)
        tiles[1][...] = jnp.zeros_like(tiles[1])

        def step(j, _):
            if acts is acts0:
                tok_load(j).wait()
            for side in range(2):
                n = 2 * j + side
                weave(acts(tiles[side], n), sums(tiles[1 - side], (n + 2 * count - 1) % (2 * count)))
            for when, group, what in ticks:
                @pl.when(j == when)
                def _():
                    tick(group, what)
            return 0

        lax.fori_loop(0, count, step, 0)
        for last in sums(tiles[1], 2 * count - 1):
            last()

    def put(block, value):
        part[SLOT[block]:SLOT[block] + 128, :] = value * scale

    def block_of(r, c):
        return slice(128 * r, 128 * r + 128), slice(128 * c, 128 * c + 128)

    def put_h(b, k, first):
        for r, c in KEPT["H"]:
            at = first + 128 * r
            put(("H", b, r, c), (acc_a if c > 1 else acc_b)[k, at:at + 128, 128 * (c % 2):128 * (c % 2) + 128])

    def put_left(b):
        for r, c in KEPT["S"]:
            rows_at, cols_at = block_of(r - 2 * (c > 1), c % 2)
            put(("S", b, r, c), (acc_b if c > 1 else acc_a)[0, rows_at, cols_at])
        for c in range(4):
            rows_at, cols_at = block_of(4 - 2 * (c > 1), c % 2)
            put(("U", b, 0, c), (acc_b if c > 1 else acc_a)[0, rows_at, cols_at])
        put(("A", b, 0, 0), acc_c[0:128, 0:128])
        put(("Q", b, 0, 0), acc_c[128:256, 128:256])

    barrier = pltpu.get_barrier_semaphore()
    for d in "cxyz":
        pl.semaphore_signal(barrier, inc=1, device_id=(peer[d],), device_id_type=MESH)
    for n in range(count):
        tok_load(n).start()
    og_load.start()
    wut[0] = wu[0].T
    wut[1] = wu[1].T
    wdt[...] = wd[0].T

    phase(acts0, lambda tile, n: sums0(tile), ())
    put_h(0, 0, 0)
    pl.semaphore_wait(barrier, 4)
    tick(0, 0)
    og_load.wait()

    phase(acts1, lambda tile, n: sums1(tile), ((0, 0, 1), (2, 0, 2), (3, 0, 3), (4, 0, 4), (5, 0, 5), (6, 0, 6), (7, 0, 7)))
    put_left(1)
    put_h(1, 1, 128)
    for c in range(4):
        acc = acc_a if c > 1 else acc_b
        put(("D", 1, 0, c), acc[1, 0:128, 128 * (c % 2):128 * (c % 2) + 128])
    tick(1, 0)
    tick(0, 8)

    phase(acts2, sums2, ((2, 1, 1), (6, 1, 2)))
    for load in late_loads:
        load.start()
    put_left(0)
    for c in range(4):
        put(("D", 0, 0, c), acc_d[:, 128 * c:128 * c + 128])
    tick(2, 0)

    keep = rho[0]
    fresh = 1.0 - keep

    def sum_of(block):
        return total[SLOT[block]:SLOT[block] + 128, :]

    def held(n, b):
        at = place(n, b)
        return slope0[at[0], at[1]]

    def blend(n, b, r, c, value):
        rows_at, cols_at = block_of(r, c)
        at = place(n, b)
        old = slope0[rows_at, at[1].start + 128 * c:at[1].start + 128 * c + 128]
        res[n + 2][b, rows_at, cols_at] = keep * old + fresh * value

    def symmetric(kind, n, b):
        for r, c in KEPT[kind]:
            value = sum_of((kind, b, r, c))
            blend(n, b, r, c, value)
            if r != c:
                blend(n, b, c, r, value.T)

    def precondition(b):
        grad = jnp.concatenate([sum_of(("U", b, 0, c)) for c in range(4)], axis=1)
        res[0][b] = fine(fine(held(4, b), grad, 1, 0), held(5, b), 1, 0)
        grad = jnp.concatenate([sum_of(("D", b, 0, c)) for c in range(4)], axis=1)
        res[1][b] = fine(held(7, b), fine(grad, held(6, b), 1, 1), 0, 0).T

    for step in range(1, 6):
        tick(1, step + 2)
        tick(2, step)
    tick(1, 8)
    tick(2, 6)
    for load in late_loads:
        load.wait()
    symmetric("H", 2, 0)
    tick(2, 7)
    blend(0, 1, 0, 0, sum_of(("A", 1, 0, 0)))
    blend(3, 1, 0, 0, sum_of(("Q", 1, 0, 0)))
    symmetric("S", 1, 1)
    symmetric("H", 2, 1)
    precondition(1)
    tick(2, 8)
    blend(0, 0, 0, 0, sum_of(("A", 0, 0, 0)))
    blend(3, 0, 0, 0, sum_of(("Q", 0, 0, 0)))
    symmetric("S", 1, 0)
    precondition(0)
    stores = [pltpu.make_async_copy(src, dst, out_sem.at[n]) for n, (src, dst) in enumerate(zip(res, outs))]
    for store in stores:
        store.start()
    for piece in range(len(PIECES)):
        for stage in range(4):
            halving(piece, stage).wait_send()
            doubling(piece, stage).wait_send()
    for store in stores:
        store.wait()


def solution(mesh):
    axis_size = mesh.shape["data"]

    def local_step(tokens, out_grad, w_up, w_down, a_up_old, s_up_old, a_down_old, s_down_old,
                   a_up_inv, s_up_inv, a_down_inv, s_down_inv, factor_decay):
        rows = tokens.shape[0]
        count = rows // (2 * TILE)
        small, wide = (2, 128, 128), (2, 512, 512)
        out_shapes = ((2, 128, 512), (2, 512, 128), small, wide, wide, small)

        def kernel(tok, og, wu, wd, rho, *refs):
            body(axis_size, rows, tok, og, wu, wd, rho, refs[0:4], refs[4:8], refs[8:14],
                 *refs[14:19], refs[19:21], *refs[21:30], refs[30:36], *refs[36:])

        anywhere = pl.BlockSpec(memory_space=pl.ANY)
        inside = pl.BlockSpec(memory_space=pltpu.VMEM)
        half = lambda *shape: pltpu.VMEM(shape, BF)
        full = lambda *shape: pltpu.VMEM(shape, F32)
        sems = pltpu.SemaphoreType.DMA
        return tuple(pl.pallas_call(
            kernel,
            in_specs=[anywhere] * 2 + [inside] * 2 + [pl.BlockSpec(memory_space=pltpu.SMEM)] + [anywhere] * 8,
            out_specs=[anywhere] * 6,
            out_shape=[jax.ShapeDtypeStruct(s, F32) for s in out_shapes],
            scratch_shapes=[half(rows, 128), half(rows, 128), half(512, rows), full(512, rows), half(128, rows),
                            half(1280, TILE), half(1280, TILE), half(2, 512, 128), half(128, 512),
                            full(2, 640, 256), full(2, 384, 256), full(256, 256), full(128, 512),
                            full(TOTAL_ROWS, 128), full(TOTAL_ROWS - TOTAL_ROWS // 16, 128), full(TOTAL_ROWS, 128)]
            + [full(*s) for s in out_shapes]
            + [sems((count + 17,)), sems((6,)), sems((2, 4, len(PIECES))), sems((2, 4, len(PIECES)))],
            compiler_params=pltpu.CompilerParams(vmem_limit_bytes=63 * 2**20, collective_id=0, has_side_effects=True),
        )(tokens, out_grad, w_up, w_down, factor_decay.reshape(1), a_up_old, s_up_old, a_down_old, s_down_old,
          a_up_inv, s_up_inv, a_down_inv, s_down_inv))

    batch_spec = P("data", None)
    return jax.shard_map(local_step, mesh=mesh, in_specs=(batch_spec, batch_spec) + (P(),) * 11,
                         out_specs=(P(),) * 6, check_vma=False)
```

profile of v0, /device:TPU:0, one launch (start us, length us, event | category | flops | bytes accessed | tf_op | source)
XLA Modules:
  0.0 98.9 jit_solution(5797533737147520797)
XLA Ops:
  1.3 87.8 %shard_map.172 = (f32[2,128,512]{2,1,0:T(8,128)}, f32[2,512,128]{2,1,0:T(8,128)}, f32[2,128,128]{2,1,0:T(8,128)}, f32[2,512,512]{2,1,0:T(8,128)}, f32[2,512,512]{2,1,0:T(8,128)}, /*index=5*/f32[2,128,128]{2,1,0:T(8,128)}) custom-call(bf16[8192,128]{1,0:T(8,128)(2,1)} %tok.1, bf16[8192,128]{1,0:T(8,128)(2,1)} %og.1, bf16[2,128,512]{2,1,0:T(8,128)(2,1)} %wu.1, ...), custom_call_target="tpu_custom_call" | custom-call | tf_op jit(solution)/shard_map/pallas_call | solution.py:417
  89.1 0.0 copy-start.1
  89.1 2.0 %copy.26 = f32[2,128,512]{2,1,0:T(8,128)} copy(f32[2,128,512]{2,1,0:T(8,128)} %get-tuple-element.12) | data formatting | bytes 1048576
  91.2 1.9 %copy.27 = f32[2,512,128]{2,1,0:T(8,128)} copy(f32[2,512,128]{2,1,0:T(8,128)} %get-tuple-element.13) | data formatting | bytes 1048576
  93.0 1.6 %copy.28 = f32[2,128,128]{2,1,0:T(8,128)} copy(f32[2,128,128]{2,1,0:T(8,128)} %get-tuple-element.14) | data formatting | bytes 262144
  94.6 0.0 copy-done.1
  94.6 0.0 copy-start
  94.6 1.3 %copy.29 = f32[2,512,512]{2,1,0:T(8,128)} copy(f32[2,512,512]{2,1,0:T(8,128)S(1)} %copy-done.1) | data formatting | bytes 4194304
  95.9 1.0 %copy-done = f32[2,512,512]{2,1,0:T(8,128)S(1)} copy-done((f32[2,512,512]{2,1,0:T(8,128)S(1)}, f32[2,512,512]{2,1,0:T(8,128)}, u32[]{:S(2)}) %copy-start) | copy-done | bytes 2097176
  96.9 0.0 copy-start.2
  96.9 1.3 %copy.30 = f32[2,512,512]{2,1,0:T(8,128)} copy(f32[2,512,512]{2,1,0:T(8,128)S(1)} %copy-done) | data formatting | bytes 4194304
  98.3 0.0 copy-done.2
  98.3 0.7 copy.31
Async XLA Ops:
  89.1 5.5 %copy-start.1 = (f32[2,512,512]{2,1,0:T(8,128)S(1)}, f32[2,512,512]{2,1,0:T(8,128)}, u32[]{:S(2)}) copy-start(f32[2,512,512]{2,1,0:T(8,128)} %get-tuple-element.15) | copy-start | bytes 6291460
  94.6 2.3 %copy-start = (f32[2,512,512]{2,1,0:T(8,128)S(1)}, f32[2,512,512]{2,1,0:T(8,128)}, u32[]{:S(2)}) copy-start(f32[2,512,512]{2,1,0:T(8,128)} %get-tuple-element.16) | copy-start | bytes 6291460
  96.9 1.3 %copy-start.2 = (f32[2,128,128]{2,1,0:T(8,128)S(1)}, f32[2,128,128]{2,1,0:T(8,128)}, u32[]{:S(2)}) copy-start(f32[2,128,128]{2,1,0:T(8,128)} %get-tuple-element.17) | copy-start | bytes 393220
where the time goes:
time: 99.2 us; the launch traced here: 98.9 us
  Pallas kernels  87.8 us (89%)
  local copies, waits for them, and re-layouts  9.78 us (10%)
  between operations  1.31 us (1%)
    pallas_call x1, Pallas kernels, local_step(): pl.pallas_call(kernel, in_specs=[anywhere] * 2 + [inside] * 2 + [pl.Block...  87.8 us
    unnamed x12, local copies, waits for them, and re-layouts  9.78 us

commit v1 on v0

v1 whole, which is shorter than its diff:
```python
import jax
import jax.numpy as jnp
from jax import lax
from jax.experimental import pallas as pl
from jax.experimental.pallas import tpu as pltpu
from jax.sharding import PartitionSpec as P

BF = jnp.bfloat16
F32 = jnp.float32
MESH = pl.DeviceIdType.MESH
HIGH = lax.Precision.HIGHEST
C0 = 0.7978845608028654
CA = C0 * 0.044715
TILE = 512
CHUNK = 256
STRIDE = {"c": 1, "x": 2, "y": 4, "z": 8}
ORDERS = ("cxyz", "cyzx", "czxy")

LOWER = [(r, c) for c in range(4) for r in range(c, 4)]
MIXED = [(0, 0), (1, 0), (1, 1), (2, 2), (3, 2), (3, 3), (0, 2), (1, 2), (0, 3), (1, 3)]
KEPT = {("S", 0): LOWER, ("S", 1): LOWER, ("H", 0): LOWER, ("H", 1): MIXED}


def tri(kind, b):
    return [(kind, b, r, c) for r, c in KEPT[(kind, b)]]


def row(kind, b):
    return [(kind, b, 0, c) for c in range(4)]


GROUPS = (
    (6, row("D", 1) + [("A", 0, 0, 0), ("Q", 1, 0, 0)] + tri("H", 0) + tri("H", 1)),
    (6, row("U", 1) + row("D", 0) + [("A", 1, 0, 0), ("Q", 0, 0, 0)] + tri("S", 1)),
    (6, row("U", 0) + tri("S", 0)),
)
SLOT = {}
PIECES = []
GROUP_PIECES = []
for _count, _blocks in GROUPS:
    _members = []
    for _n in range(_count):
        _size = -(-len(_blocks) // (_count - _n))
        _members.append(len(PIECES))
        PIECES.append((ORDERS[_n % 3], 128 * len(SLOT), 128 * _size))
        for _block in _blocks[:_size]:
            SLOT[_block] = 128 * len(SLOT)
        _blocks = _blocks[_size:]
    GROUP_PIECES.append(_members)
TOTAL_ROWS = 128 * len(SLOT)


def mm(a, b):
    return lax.dot_general(a, b, (((1,), (0,)), ((), ())), preferred_element_type=F32)


def nt(a, b):
    return lax.dot_general(a, b, (((1,), (1,)), ((), ())), preferred_element_type=F32)


def fine(a, b, ca, cb):
    return lax.dot_general(a, b, (((ca,), (cb,)), ((), ())), precision=HIGH, preferred_element_type=F32)


def rounded(x):
    return x.astype(BF).astype(F32)


def gelu_parts(z):
    sq = z * z
    cub = CA * sq
    base = cub + C0
    half = 0.5 * jnp.tanh(z * base) + 0.5
    return cub, base, half


def gelu(z):
    return z * gelu_parts(z)[2]


def gelu_slope(z):
    cub, base, half = gelu_parts(z)
    return half + (z * half) * ((base + (cub + cub)) * (2.0 - (half + half)))


def weave(first, second):
    done = 0
    for n, step in enumerate(first):
        step()
        while done < len(second) and (done + 1) * len(first) <= (n + 1) * len(second):
            second[done]()
            done += 1
    for step in second[done:]:
        step()


def body(axis_size, rows, tok_hbm, og_hbm, wu, wd, rho, old_hbm, inv_hbm, outs,
         tok, og, pre0, pre1, hid0, mid, grad0, tiles, wut, wdt, acc_a, acc_b, acc_c, acc_d, part, recv, total, new, invs, res,
         load_sem, out_sem, send_sem, recv_sem):
    me = lax.axis_index("data")
    bit = {d: (me // s) % 2 for d, s in STRIDE.items()}
    peer = {d: me + s - 2 * s * bit[d] for d, s in STRIDE.items()}
    count = rows // (2 * TILE)
    scale = 1.0 / (axis_size * rows)

    def tok_load(n):
        here = pl.ds(pl.multiple_of(n * (2 * TILE), 2 * TILE), 2 * TILE)
        return pltpu.make_async_copy(tok_hbm.at[here, :], tok.at[here, :], load_sem.at[n])

    def og_load(n):
        here = pl.ds(pl.multiple_of(n * (2 * TILE), 2 * TILE), 2 * TILE)
        return pltpu.make_async_copy(og_hbm.at[here, :], og.at[here, :], load_sem.at[count + n])

    late_loads = [pltpu.make_async_copy(src, dst, load_sem.at[2 * count + n])
                  for n, (src, dst) in enumerate(zip(tuple(old_hbm) + tuple(inv_hbm), tuple(new) + tuple(invs)))]

    def spot(piece, stage):
        order, base, size = PIECES[piece]
        at = base
        for s in range(stage):
            at = at + bit[order[s]] * (size >> (s + 1))
        return at

    def inbox(piece, stage):
        _, base, size = PIECES[piece]
        return base - base // 16 + sum(size >> (s + 1) for s in range(stage))

    def halving(piece, stage):
        order, _, size = PIECES[piece]
        half = size >> (stage + 1)
        away = pl.multiple_of(spot(piece, stage) + (1 - bit[order[stage]]) * half, 8)
        return pltpu.make_async_remote_copy(
            src_ref=part.at[pl.ds(away, half), :], dst_ref=recv.at[pl.ds(inbox(piece, stage), half), :],
            send_sem=send_sem.at[0, stage, piece], recv_sem=recv_sem.at[0, stage, piece],
            device_id=(peer[order[stage]],), device_id_type=MESH)

    def doubling(piece, stage):
        order, _, size = PIECES[piece]
        half = size >> (stage + 1)
        at = pl.multiple_of(spot(piece, stage + 1), 8)
        return pltpu.make_async_remote_copy(
            src_ref=total.at[pl.ds(at, half), :], dst_ref=total.at[pl.ds(at, half), :],
            send_sem=send_sem.at[1, stage, piece], recv_sem=recv_sem.at[1, stage, piece],
            device_id=(peer[order[stage]],), device_id_type=MESH)

    def tick(group, step):
        for piece in GROUP_PIECES[group]:
            order, _, size = PIECES[piece]
            if step == 0:
                halving(piece, 0).start()
            elif step < 4:
                stage = step - 1
                halving(piece, stage).wait_recv()
                at, box, half = spot(piece, step), inbox(piece, stage), size >> (step + 1)
                keep = bit[order[step]] * half
                for shift in (half - keep, keep):
                    here = pl.ds(pl.multiple_of(at + shift, 8), half)
                    there = pl.ds(pl.multiple_of(box + shift, 8), half)
                    part[here, :] = part[here, :] + recv[there, :]
                halving(piece, step).start()
            elif step == 4:
                halving(piece, 3).wait_recv()
                box, half = inbox(piece, 3), size >> 4
                here = pl.ds(pl.multiple_of(spot(piece, 4), 8), half)
                total[here, :] = part[here, :] + recv[box:box + half, :]
                doubling(piece, 3).start()
            else:
                doubling(piece, 8 - step).wait_recv()
                if step < 8:
                    doubling(piece, 7 - step).start()

    def near(n):
        return pl.ds(pl.multiple_of(n * TILE, TILE), TILE)

    def chunks(make):
        return [make(f) for f in range(0, 512, CHUNK)]

    def acts0(tile, n):
        kept = {}

        def start():
            kept["u"] = tok[near(n), :].T
            tile[512:640, :] = kept["u"]
            tile[640:768, :] = og[near(n), :].T

        def first(f):
            def step():
                pre = mm(wut[0, f:f + CHUNK, :], kept["u"]).astype(BF)
                pre0[f:f + CHUNK, near(n)] = pre
                hid = gelu(pre.astype(F32)).astype(BF)
                tile[f:f + CHUNK, :] = hid
                hid0[f:f + CHUNK, near(n)] = hid
            return step

        def middle():
            kept["m"] = mm(wdt[...], tile[0:512, :]).astype(BF)
            mid[:, near(n)] = kept["m"]

        def second(f):
            def step():
                pre = mm(wut[1, f:f + CHUNK, :], kept["m"]).astype(BF)
                pre1[f:f + CHUNK, near(n)] = pre
                tile[768 + f:768 + f + CHUNK, :] = gelu(pre.astype(F32)).astype(BF)
            return step

        return [start] + chunks(first) + [middle] + chunks(second)

    def left_sums(tile, k, size):
        def one():
            acc_a[k, 0:size, :] += nt(tile[0:size, :], tile[0:256, :])

        def two():
            acc_b[k, 0:size - 256, :] += nt(tile[256:size, :], tile[256:512, :])

        return [one, two]

    def narrow_sums(tile):
        def one():
            acc_c[...] += nt(tile[512:768, :], tile[512:768, :])

        return [one]

    def sums0(tile, n):
        def one():
            acc_a[1] += nt(tile[640:1280, :], tile[1024:1280, :])

        def two():
            acc_b[1] += nt(tile[640:1024, :], tile[768:1024, :])

        return left_sums(tile, 0, 512) + narrow_sums(tile) + [one, two]

    def acts1(tile, n):
        kept = {}

        def start():
            kept["q"] = og[near(n), :].T
            tile[512:640, :] = mid[:, near(n)]

        def chunk(f):
            def step():
                back = rounded(mm(wd[1, f:f + CHUNK, :], kept["q"]))
                tile[f:f + CHUNK, :] = (back * gelu_slope(pre1[f:f + CHUNK, near(n)].astype(F32))).astype(BF)
            return step

        def end():
            grad = mm(wu[1], tile[0:512, :]).astype(BF)
            tile[640:768, :] = grad
            grad0[:, near(n)] = grad

        return [start] + chunks(chunk) + [end]

    def sums1(tile, n):
        def one():
            acc_d[...] += nt(tile[640:768, :], hid0[:, near(n)])

        return left_sums(tile, 0, 640) + narrow_sums(tile) + [one]

    def acts2(tile, n):
        def start():
            tile[512:640, :] = tok[near(n), :].T

        def chunk(f):
            def step():
                back = rounded(mm(wd[0, f:f + CHUNK, :], grad0[:, near(n)]))
                tile[f:f + CHUNK, :] = (back * gelu_slope(pre0[f:f + CHUNK, near(n)].astype(F32))).astype(BF)
            return step

        return [start] + chunks(chunk)

    def sums2(tile, n):
        return left_sums(tile, 0, 640)

    def phase(acts, sums, ticks):
        for acc in (acc_a, acc_b, acc_c, acc_d):
            acc[...] = jnp.zeros_like(acc)
        tiles[1][...] = jnp.zeros_like(tiles[1])

        def step(j, _):
            if acts is acts0:
                tok_load(j).wait()
                og_load(j).wait()
            for side in range(2):
                n = 2 * j + side
                weave(acts(tiles[side], n), sums(tiles[1 - side], (n + 2 * count - 1) % (2 * count)))
            for when, group, what in ticks:
                @pl.when(j == when)
                def _():
                    tick(group, what)
            return 0

        lax.fori_loop(0, count, step, 0)
        for last in sums(tiles[1], 2 * count - 1):
            last()

    def put(block, value):
        part[SLOT[block]:SLOT[block] + 128, :] = value * scale

    def block_of(r, c):
        return slice(128 * r, 128 * r + 128), slice(128 * c, 128 * c + 128)

    def put_left(kind, b):
        for r, c in LOWER:
            rows_at, cols_at = block_of(r - 2 * (c > 1), c % 2)
            put((kind, b, r, c), (acc_b if c > 1 else acc_a)[0, rows_at, cols_at])
        if kind == "S":
            for c in range(4):
                rows_at, cols_at = block_of(4 - 2 * (c > 1), c % 2)
                put(("U", b, 0, c), (acc_b if c > 1 else acc_a)[0, rows_at, cols_at])

    def put_right(b):
        for r, c in MIXED:
            rows_at, cols_at = block_of(r + 1, c % 2)
            put(("H", b, r, c), (acc_a if c > 1 else acc_b)[1, rows_at, cols_at])
        for c in range(4):
            rows_at, cols_at = block_of(0, c % 2)
            put(("D", b, 0, c), (acc_a if c > 1 else acc_b)[1, rows_at, cols_at])

    barrier = pltpu.get_barrier_semaphore()
    for d in "cxyz":
        pl.semaphore_signal(barrier, inc=1, device_id=(peer[d],), device_id_type=MESH)
    for n in range(count):
        tok_load(n).start()
        og_load(n).start()
    for load in late_loads:
        load.start()
    wut[0] = wu[0].T
    wut[1] = wu[1].T
    wdt[...] = wd[0].T

    phase(acts0, sums0, ())
    put_left("H", 0)
    put_right(1)
    put(("A", 0, 0, 0), acc_c[0:128, 0:128])
    put(("Q", 1, 0, 0), acc_c[128:256, 128:256])
    pl.semaphore_wait(barrier, 4)
    tick(0, 0)

    phase(acts1, sums1, ((1, 0, 1), (5, 0, 2)))
    put_left("S", 1)
    put(("A", 1, 0, 0), acc_c[0:128, 0:128])
    put(("Q", 0, 0, 0), acc_c[128:256, 128:256])
    for c in range(4):
        put(("D", 0, 0, c), acc_d[:, 128 * c:128 * c + 128])
    tick(1, 0)
    tick(0, 3)

    phase(acts2, sums2, ((1, 1, 1), (2, 0, 4), (4, 0, 5), (5, 1, 2), (7, 0, 6)))
    put_left("S", 0)
    tick(2, 0)

    keep = rho[0]
    fresh = 1.0 - keep

    for load in late_loads:
        load.wait()

    def sum_of(block):
        return total[SLOT[block]:SLOT[block] + 128, :]

    def blend(n, b, r, c, value):
        rows_at, cols_at = block_of(r, c)
        new[n][b, rows_at, cols_at] = keep * new[n][b, rows_at, cols_at] + fresh * value

    def symmetric(kind, n, b):
        for r, c in KEPT[(kind, b)]:
            value = sum_of((kind, b, r, c))
            blend(n, b, r, c, value)
            if r != c:
                blend(n, b, c, r, value.T)

    def narrow(kind, n, b):
        blend(n, b, 0, 0, sum_of((kind, b, 0, 0)))

    def precondition_up(b):
        grad = jnp.concatenate([sum_of(("U", b, 0, c)) for c in range(4)], axis=1)
        res[0][b] = fine(fine(invs[0][b], grad, 1, 0), invs[1][b], 1, 0)

    def precondition_down(b):
        grad = jnp.concatenate([sum_of(("D", b, 0, c)) for c in range(4)], axis=1)
        res[1][b] = fine(invs[3][b], fine(grad, invs[2][b], 1, 1), 0, 0).T

    tick(1, 3)
    tick(0, 7)
    tick(2, 1)
    tick(1, 4)
    tick(0, 8)
    tick(2, 2)
    tick(1, 5)
    symmetric("H", 2, 0)
    tick(1, 6)
    tick(2, 3)
    symmetric("H", 2, 1)
    tick(2, 4)
    tick(1, 7)
    narrow("A", 0, 0)
    narrow("Q", 3, 1)
    tick(2, 5)
    tick(1, 8)
    precondition_down(1)
    tick(2, 6)
    symmetric("S", 1, 1)
    tick(2, 7)
    narrow("A", 0, 1)
    narrow("Q", 3, 0)
    precondition_up(1)
    precondition_down(0)
    tick(2, 8)
    symmetric("S", 1, 0)
    precondition_up(0)
    stores = [pltpu.make_async_copy(src, dst, out_sem.at[n]) for n, (src, dst) in enumerate(zip(tuple(res) + tuple(new), outs))]
    for store in stores:
        store.start()
    for piece in range(len(PIECES)):
        for stage in range(4):
            halving(piece, stage).wait_send()
            doubling(piece, stage).wait_send()
    for store in stores:
        store.wait()


def solution(mesh):
    axis_size = mesh.shape["data"]

    def local_step(tokens, out_grad, w_up, w_down, a_up_old, s_up_old, a_down_old, s_down_old,
                   a_up_inv, s_up_inv, a_down_inv, s_down_inv, factor_decay):
        rows = tokens.shape[0]
        count = rows // (2 * TILE)
        small, wide = (2, 128, 128), (2, 512, 512)
        out_shapes = ((2, 128, 512), (2, 512, 128), small, wide, wide, small)

        def kernel(tok, og, wu, wd, rho, *refs):
            body(axis_size, rows, tok, og, wu, wd, rho, refs[0:4], refs[4:8], refs[8:14],
                 *refs[14:21], refs[21:23], *refs[23:32], refs[32:36], refs[36:40], refs[40:42], *refs[42:])

        anywhere = pl.BlockSpec(memory_space=pl.ANY)
        inside = pl.BlockSpec(memory_space=pltpu.VMEM)
        half = lambda *shape: pltpu.VMEM(shape, BF)
        full = lambda *shape: pltpu.VMEM(shape, F32)
        sems = pltpu.SemaphoreType.DMA
        return tuple(pl.pallas_call(
            kernel,
            in_specs=[anywhere] * 2 + [inside] * 2 + [pl.BlockSpec(memory_space=pltpu.SMEM)] + [anywhere] * 8,
            out_specs=[anywhere] * 6,
            out_shape=[jax.ShapeDtypeStruct(s, F32) for s in out_shapes],
            scratch_shapes=[half(rows, 128), half(rows, 128), half(512, rows), half(512, rows), half(512, rows), half(128, rows),
                            half(128, rows), half(1280, TILE), half(1280, TILE), half(2, 512, 128), half(128, 512),
                            full(2, 640, 256), full(2, 384, 256), full(256, 256), full(128, 512),
                            full(TOTAL_ROWS, 128), full(TOTAL_ROWS - TOTAL_ROWS // 16, 128), full(TOTAL_ROWS, 128)]
            + [full(*s) for s in out_shapes[2:]] * 2 + [full(*s) for s in out_shapes[:2]]
            + [sems((2 * count + 8,)), sems((6,)), sems((2, 4, len(PIECES))), sems((2, 4, len(PIECES)))],
            compiler_params=pltpu.CompilerParams(vmem_limit_bytes=63 * 2**20, collective_id=0, has_side_effects=True),
        )(tokens, out_grad, w_up, w_down, factor_decay.reshape(1), a_up_old, s_up_old, a_down_old, s_down_old,
          a_up_inv, s_up_inv, a_down_inv, s_down_inv))

    batch_spec = P("data", None)
    return jax.shard_map(local_step, mesh=mesh, in_specs=(batch_spec, batch_spec) + (P(),) * 11,
                         out_specs=(P(),) * 6, check_vma=False)
```

time: 99.2 us -> 105 us (1.058)
  Pallas kernels: 87.8 us -> 93.3 us
    pallas_call x1, Pallas kernels: 87.8 us -> 93.3 us  [local_step(): pl.pallas_call(kernel, in_specs=[anywhere] * 2 + [inside] * 2 + [pl.Block...]
where the time goes in v1:
time: 105 us; the launch traced here: 104 us
  Pallas kernels  93.3 us (89%)
  local copies, waits for them, and re-layouts  9.78 us (9%)
  between operations  1.31 us (1%)
    pallas_call x1, Pallas kernels, local_step(): pl.pallas_call(kernel, in_specs=[anywhere] * 2 + [inside] * 2 + [pl.Block...  93.3 us
    unnamed x12, local copies, waits for them, and re-layouts  9.78 us

profile of v1, /device:TPU:0, one launch (start us, length us, event | category | flops | bytes accessed | tf_op | source)
XLA Modules:
  0.0 104.4 jit_solution(12639623389557677947)
XLA Ops:
  1.3 93.3 %shard_map.172 = (f32[2,128,512]{2,1,0:T(8,128)}, f32[2,512,128]{2,1,0:T(8,128)}, f32[2,128,128]{2,1,0:T(8,128)}, f32[2,512,512]{2,1,0:T(8,128)}, f32[2,512,512]{2,1,0:T(8,128)}, /*index=5*/f32[2,128,128]{2,1,0:T(8,128)}) custom-call(bf16[8192,128]{1,0:T(8,128)(2,1)} %tok.1, bf16[8192,128]{1,0:T(8,128)(2,1)} %og.1, bf16[2,128,512]{2,1,0:T(8,128)(2,1)} %wu.1, ...), custom_call_target="tpu_custom_call" | custom-call | tf_op jit(solution)/shard_map/pallas_call | solution.py:440
  94.6 0.0 copy-start.1
  94.6 2.0 %copy.26 = f32[2,128,512]{2,1,0:T(8,128)} copy(f32[2,128,512]{2,1,0:T(8,128)} %get-tuple-element.12) | data formatting | bytes 1048576
  96.6 1.9 %copy.27 = f32[2,512,128]{2,1,0:T(8,128)} copy(f32[2,512,128]{2,1,0:T(8,128)} %get-tuple-element.13) | data formatting | bytes 1048576
  98.5 1.6 %copy.28 = f32[2,128,128]{2,1,0:T(8,128)} copy(f32[2,128,128]{2,1,0:T(8,128)} %get-tuple-element.14) | data formatting | bytes 262144
  100.1 0.0 copy-done.1
  100.1 0.0 copy-start
  100.1 1.3 %copy.29 = f32[2,512,512]{2,1,0:T(8,128)} copy(f32[2,512,512]{2,1,0:T(8,128)S(1)} %copy-done.1) | data formatting | bytes 4194304
  101.4 1.0 copy-done
  102.4 0.0 copy-start.2
  102.4 1.3 %copy.30 = f32[2,512,512]{2,1,0:T(8,128)} copy(f32[2,512,512]{2,1,0:T(8,128)S(1)} %copy-done) | data formatting | bytes 4194304
  103.7 0.0 copy-done.2
  103.7 0.7 copy.31
Async XLA Ops:
  94.6 5.5 %copy-start.1 = (f32[2,512,512]{2,1,0:T(8,128)S(1)}, f32[2,512,512]{2,1,0:T(8,128)}, u32[]{:S(2)}) copy-start(f32[2,512,512]{2,1,0:T(8,128)} %get-tuple-element.15) | copy-start | bytes 6291460
  100.1 2.3 %copy-start = (f32[2,512,512]{2,1,0:T(8,128)S(1)}, f32[2,512,512]{2,1,0:T(8,128)}, u32[]{:S(2)}) copy-start(f32[2,512,512]{2,1,0:T(8,128)} %get-tuple-element.16) | copy-start | bytes 6291460
  102.4 1.3 %copy-start.2 = (f32[2,128,128]{2,1,0:T(8,128)S(1)}, f32[2,128,128]{2,1,0:T(8,128)}, u32[]{:S(2)}) copy-start(f32[2,128,128]{2,1,0:T(8,128)} %get-tuple-element.17) | copy-start | bytes 393220
